TPU v7x, 32 devices: a whole 2x2x4 slice. The times are simulated.
32 devices in a mesh: parts: 2 (over x), rows: 16 (over z, y, core).
Axes of the slice: x: 2, y: 2, z: 4, core: 2. Of those that a mesh axis runs over, the one named last changes fastest.
Arguments:
- feature_bin: int32 [16384, 700], P(('parts', 'rows')), parts along dimension 0, may hold values from 0 to 255
- doc_leaf: int32 [16384], P(('parts', 'rows')), parts along dimension 0, may hold values from 0 to 31
- current_score: float32 [16384], P(('parts', 'rows')), parts along dimension 0, may hold values from -8 to 8
- relevance: int32 [16384], P(('parts', 'rows')), parts along dimension 0, may hold values from 0 to 4
- doc_rank: int32 [16384], P(('parts', 'rows')), parts along dimension 0, may hold values from 0 to 255, as said below
- query_length: int32 [64], P(('parts', 'rows')), parts along dimension 0, may hold values from 10 to 256, as said below
- feature_votes: int32 [32, 32, 20], P(('parts', 'rows')), parts along dimension 0, may hold values from 0 to 699, all different within a row
- elected: int32 [64, 40], P('parts'), parts along dimension 0, may hold values from 0 to 699, all different within a row
Outputs:
- gradient: float32 [16384], P(('parts', 'rows')), parts along dimension 0
- hessian: float32 [16384], P(('parts', 'rows')), parts along dimension 0
- vote_count: int32 [64, 700], P('parts'), parts along dimension 0
- split_gain: float32 [64, 40, 256], P('parts'), parts along dimension 0
There are 2 independent parts, one for each index of `parts`. A program takes and returns all parts, laid end to end along the dimension named above; each array names one. Nothing has to cross between parts.
Inputs may be any that keep to these rules, and one draw needn't show every extreme that they name: `query_length`: query q holds slots q * 256 to (q + 1) * 256 - 1 of the document arrays; in every draw some query has exactly 256 documents. `doc_rank`: within each query the live documents hold positions 0 to query_length - 1, each once; slots that are not live hold positions from query_length to 255. `feature_votes`: the 20 votes of one device for one leaf are different features. The 40 elected features of one leaf are different.
All inputs are finite; a program needn't handle non-finite values.
Results may differ from a plain program's by a relative error of at most 0.0003.
Values sent between devices are 32-bit elements; how exact they have to be, the bound alone decides.
No kernel may reach another device: no remote copies, remote signals or barrier semaphores. Data moves between devices by JAX's collectives and lax.ppermute only.
A program may use at most 64 MiB of HBM per device.

v0:
```python
import math
import jax
import jax.numpy as jnp
from jax import lax
from jax.sharding import PartitionSpec as P

B = 256
QMAX = 256
ridge_weight = 1.0


def query_terms(scores, levels, places, length):
    positions = jnp.arange(scores.shape[0], dtype=jnp.int32)
    living = positions < length
    gains = jnp.exp2(levels.astype(jnp.float32)) - 1.0
    discount = 1.0 / jnp.log2(places.astype(jnp.float32) + 2.0)
    higher = (levels[None, :] > levels[:, None]) & living[None, :]
    earlier = (
        (levels[None, :] == levels[:, None])
        & (positions[None, :] < positions[:, None])
        & living[None, :]
    )
    ideal_place = jnp.sum((higher | earlier).astype(jnp.float32), axis=1)
    ideal = jnp.sum(jnp.where(living, gains / jnp.log2(ideal_place + 2.0), 0.0))
    scaling = 1.0 / jnp.maximum(ideal, 1.0)
    ordered = (levels[:, None] > levels[None, :]) & living[:, None] & living[None, :]
    chance = jax.nn.sigmoid(scores[None, :] - scores[:, None])
    change = (
        (gains[:, None] - gains[None, :]) * jnp.abs(discount[:, None] - discount[None, :]) * scaling
    )
    pushes = jnp.where(ordered, chance * change, 0.0)
    curves = jnp.where(ordered, chance * (1.0 - chance) * change, 0.0)
    return (
        jnp.sum(pushes, axis=0) - jnp.sum(pushes, axis=1),
        jnp.sum(curves, axis=0) + jnp.sum(curves, axis=1),
    )


def build_histogram(feature_bin, doc_leaf, gradient, hessian, elected, bins):
    leaves, picked = elected.shape
    documents = feature_bin.shape[0]
    leaf_hot = (doc_leaf[:, None] == jnp.arange(leaves, dtype=jnp.int32)[None, :]).astype(
        jnp.float32
    )
    columns = jnp.dot(
        leaf_hot, elected.astype(jnp.float32), precision=lax.Precision.HIGHEST
    ).astype(jnp.int32)
    chosen = jnp.take_along_axis(feature_bin, columns, axis=1)
    weighted = jnp.concatenate([leaf_hot * gradient[:, None], leaf_hot * hessian[:, None]], axis=1)
    block_rows = math.gcd(documents, 512)
    block_count = documents // block_rows
    bin_ids = jnp.arange(bins, dtype=jnp.int32)

    def add_block(index, total):
        onehot = (chosen[:, :, None] == bin_ids[None, None, :]).astype(jnp.float32)
        onehot = onehot.reshape(block_rows, picked * bins)
        return total + jnp.dot(weighted.T, onehot, precision=lax.Precision.HIGHEST)

    empty = jnp.zeros((2 * leaves, picked * bins), jnp.float32)
    total = lax.fori_loop(0, block_count, add_block, empty)
    return total.reshape(2, leaves, picked, bins)


def split_score(prefix, whole):
    remain = whole - prefix
    return (
        prefix[0] * prefix[0] / (prefix[1] + ridge_weight)
        + remain[0] * remain[0] / (remain[1] + ridge_weight)
        - whole[0] * whole[0] / (whole[1] + ridge_weight)
    )


def count_votes(feature_votes, features):
    hits = feature_votes[..., None] == jnp.arange(features, dtype=jnp.int32)
    return jnp.sum(hits.astype(jnp.int32), axis=(0, 2))


def on_device(
    feature_bin, doc_leaf, current_score, relevance, doc_rank, query_length, feature_votes, elected
):
    features = feature_bin.shape[1]
    all_votes = lax.all_gather(feature_votes, "rows", axis=0, tiled=True)
    vote_count = count_votes(all_votes, features)

    def one_query(items):
        return query_terms(items[0], items[1], items[2], items[3])

    gradient, hessian = lax.map(
        one_query,
        (
            current_score.reshape(-1, QMAX),
            relevance.reshape(-1, QMAX),
            doc_rank.reshape(-1, QMAX),
            query_length,
        ),
    )
    gradient = gradient.reshape(-1)
    hessian = hessian.reshape(-1)
    histogram = build_histogram(feature_bin, doc_leaf, gradient, hessian, elected, B)
    summed = lax.psum(histogram, "rows")
    prefix = jnp.cumsum(summed, axis=3)
    whole = jnp.sum(summed, axis=3, keepdims=True)
    split_gain = split_score(prefix, whole)
    return (gradient, hessian, vote_count, split_gain)


def solution(mesh):
    return jax.shard_map(
        on_device,
        mesh=mesh,
        in_specs=(
            P(("parts", "rows"), None),
            P(("parts", "rows")),
            P(("parts", "rows")),
            P(("parts", "rows")),
            P(("parts", "rows")),
            P(("parts", "rows")),
            P(("parts", "rows"), None, None),
            P("parts", None),
        ),
        out_specs=(
            P(("parts", "rows")),
            P(("parts", "rows")),
            P("parts", None),
            P("parts", None, None),
        ),
        check_vma=False,
    )
```

profile of v0, /device:TPU:0, one launch (start us, length us, event | category | flops | bytes accessed | tf_op | source)
XLA Modules:
  0.0 409.0 jit_solution(16073954382203800596)
XLA Ops:
  7.2 0.0 copy-start
  7.2 0.0 all-reduce.2.cloned.1.call-start
  7.3 0.8 reshape.169
  8.0 0.7 reshape.170
  8.7 0.7 reshape.171
  9.4 9.2 %while.18 = (s32[]{:T(128)}, f32[2,256]{1,0:T(2,128)S(1)}, f32[2,256]{1,0:T(2,128)S(1)}, s32[2,256]{1,0:T(2,128)S(1)}, s32[2]{0:T(128)}, /*index=5*/f32[2,256]{1...) while((s32[]{:T(128)}, f32[2,256]{1,0:T(2,128)S(1)}, f32[2,256]{1,0:T(2,128)S(1)}, ...), condition=%wide.region_7.8_spmd, body=%wide.region_0.7_spmd.sunk | while | flops 2035203 | bytes 32681 | solution.py:88
  9.5 1.2 dynamic_slice.34
  10.7 0.6 iota_compare_fusion.6
  11.4 0.2 convert_reduce_fusion.3
  11.6 1.3 exponential_add_fusion.5
  13.5 0.4 fusion.28
  14.1 1.2 dynamic_slice.34
  15.3 0.6 iota_compare_fusion.6
  16.0 0.2 convert_reduce_fusion.3
  16.2 1.3 exponential_add_fusion.5
  18.2 0.4 fusion.28
  18.6 0.0 copy-start.3
  18.7 0.0 copy-start.4
  18.7 1.0 bitcast_or_fusion
  19.7 0.1 copy.34
  19.8 0.2 reshape.179
  20.0 0.0 copy-done
  20.0 0.0 copy-start.5
  20.0 163.1 %gather_fusion = s32[20480]{0:T(1024)S(1)} fusion(s32[512,700]{0,1:T(8,128)S(1)} %copy-done, s32[20480]{0:T(1024)S(1)} %reshape.179), kind=kCustom, calls=%fused_computation | custom fusion | bytes 327680 | tf_op jit(solution)/shard_map/jit(take_along_axis)/gather | solution.py:48
  183.1 0.2 reshape.182
  183.3 0.1 copy.35
  183.4 0.0 copy-done.3
  183.4 0.0 copy-done.4
  183.4 0.0 copy-done.5
  183.5 3.3 bitcast_compare_fusion
  186.8 11.0 %fusion.22 = f32[2,32,40,256]{3,1,2,0:T(8,128)} fusion(f32[2,32,512,1]{2,1,3,0:T(8,128)S(1)} %bitcast.69, pred[40,256,512,1]{2,1,0,3:T(32,128)(4,1)S(1)} %bitcast.68), kind=kOutput, calls=%fused_computation.56 | convolution fusion | flops 4026531840 | bytes 7995392 | tf_op jit(solution)/shard_map/while/body/eval_jaxpr/dot_general | solution.py:57
  197.9 0.0 copy-start.2
  197.9 0.0 all-reduce.2.cloned.1.call-update
  197.9 0.7 copy-done.2
  198.6 24.5 %all_gather.3 = s32[16,32,20]{1,2,0:T(8,128)S(1)} all-gather(s32[1,32,20]{1,2,0:T(8,128)S(1)} %copy.33), channel_id=1, replica_groups=mesh['parts'=2,'rows'=16] {'rows'}, dimensions={0}, use_global_device_ids=true | all-gather | bytes 43520 | tf_op jit(solution)/shard_map/all_gather | solution.py:82
  223.1 4.4 %convert_reduce_fusion.1 = s32[32,700]{1,0:T(8,128)} fusion(s32[16,32,20]{1,2,0:T(8,128)S(1)} %all_gather.3), kind=kLoop, calls=%fused_computation.25 | loop fusion | flops 21481600 | bytes 130560 | tf_op jit(solution)/shard_map/reduce_sum | solution.py:75
  227.5 74.4 %all-reduce.2.cloned.1.call-done = f32[2,32,40,256]{3,1,2,0:T(8,128)} async-done(((f32[2,32,40,256]{3,1,2,0:T(8,128)}), f32[2,32,40,256]{3,1,2,0:T(8,128)}) %all-reduce.2.cloned.1.call-update) | async-done | bytes 2621456 | tf_op jit(solution)/shard_map/psum | solution.py:100
  302.0 2.2 reduce_sum.91
  304.1 0.1 copy.40
  304.2 4.3 %reshape.175 = f32[2,32,40,2,128]{4,3,1,2,0:T(2,128)} reshape(f32[2,32,40,256]{3,1,2,0:T(8,128)} %all-reduce.2.cloned.1.call-done) | data formatting | bytes 5242880 | tf_op jit(solution)/shard_map/reshape.2
  308.5 4.8 %copy.36 = f32[2,32,40,2,128]{4,2,3,1,0:T(8,128)} copy(f32[2,32,40,2,128]{4,3,1,2,0:T(2,128)} %reshape.175) | data formatting | bytes 5242880 | tf_op jit(solution)/shard_map/reshape.2
  313.3 69.9 %reduce-window.6 = f32[2,32,40,2,128]{4,2,3,1,0:T(8,128)} reduce-window(f32[2,32,40,2,128]{4,2,3,1,0:T(8,128)} %copy.36, f32[]{:T(128)} %constant.79.clone.1), window={size=1x1x1x1x128 pad=0_0x0_0x0_0x0_0x127_0}, to_apply=%region_10.11 | reduce-window | flops 83230720 | bytes 5242884 | tf_op jit(solution)/shard_map/reduce-window
  383.1 4.0 slice.41
  387.1 2.7 copy.37
  389.8 0.2 fusion.14
  390.0 0.1 copy.38
  390.0 0.0 copy-start.1
  390.0 2.3 broadcast_add_fusion
  392.4 0.2 copy-done.1
  392.5 2.3 bitcast_subtract_fusion
  394.8 0.2 fusion.13
  395.0 1.7 copy.39
  396.7 2.3 div.58
  399.1 0.1 copy.42
  399.1 3.1 fusion.12
  (24 shorter events, 0.3 us)
Async XLA Ops:
  7.2 12.8 %copy-start = (s32[512,700]{0,1:T(8,128)S(1)}, s32[512,700]{0,1:T(8,128)}, u32[]{:S(2)}) copy-start(s32[512,700]{0,1:T(8,128)} %param.10) | copy-start | bytes 4300804
  7.2 294.8 %all-reduce.2.cloned.1.call-start = ((), (), s32[]{:S(2)}) async-start(), calls=%async_computation | async-start | bytes 5242880 | tf_op jit(solution)/shard_map/psum | solution.py:100
  18.6 164.8 %copy-start.3 = (f32[1,2,2,128]{3,1,2,0:T(2,128)}, f32[1,2,2,128]{3,1,2,0:T(2,128)S(1)}, u32[]{:S(2)}) copy-start(f32[1,2,2,128]{3,1,2,0:T(2,128)S(1)} %copy.45) | copy-start | bytes 6148
  18.7 164.8 %copy-start.4 = (f32[1,2,2,128]{3,1,2,0:T(2,128)}, f32[1,2,2,128]{3,1,2,0:T(2,128)S(1)}, u32[]{:S(2)}) copy-start(f32[1,2,2,128]{3,1,2,0:T(2,128)S(1)} %copy.46) | copy-start | bytes 6148
  20.0 163.4 %copy-start.5 = (s32[512]{0:T(512)S(1)}, s32[512]{0:T(512)}, u32[]{:S(2)}) copy-start(s32[512]{0:T(512)} %param.11) | copy-start | bytes 6148
  197.9 0.7 copy-start.2
  390.0 2.5 copy-start.1
Sparse Core Ops, SparseCore 0:
  198.0 103.8 all-reduce.1
where the time goes:
time: 417 us; the launch traced here: 409 us
  local copies, waits for them, and re-layouts  189 us (45%)
  other arithmetic  92.9 us (22%)
  waiting for transfers between devices  74.4 us (18%)
  blocking collectives  24.5 us (6%)
  between operations  14.3 us (3%)
  matrix products  12 us (3%)
    gather x5, local copies, waits for them, and re-layouts, build_histogram(): chosen = jnp.take_along_axis(feature_bin, columns, axis=1)  164 us
    psum x1, waiting for transfers between devices, on_device(): summed = lax.psum(histogram, 'rows')  74.4 us
    another operation x5, other arithmetic  72.3 us
    all_gather x1, blocking collectives, on_device(): all_votes = lax.all_gather(feature_votes, 'rows', axis=0, tiled=True)  24.5 us
    dot_general x1, matrix products, add_block(): return total + jnp.dot(weighted.T, onehot, precision=lax.Precision.HIGHEST)  11 us
    another operation x4, local copies, waits for them, and re-layouts  9.1 us
  transfers between devices with their start and end apart: 1, of which 1 were waited for; matrix products, arithmetic and copies ran while one was open for 1% of the time, Pallas kernels for 0%

commit v1 on v0

--- a/solution.py
+++ b/solution.py
@@ -97,7 +97,11 @@
     gradient = gradient.reshape(-1)
     hessian = hessian.reshape(-1)
     histogram = build_histogram(feature_bin, doc_leaf, gradient, hessian, elected, B)
-    summed = lax.psum(histogram, "rows")
+    count = lax.axis_size("rows")
+    summed, far = (histogram, 1)
+    while far < count:
+        summed = summed + lax.ppermute(summed, "rows", [(i, i ^ far) for i in range(count)])
+        far = 2 * far
     prefix = jnp.cumsum(summed, axis=3)
     whole = jnp.sum(summed, axis=3, keepdims=True)
     split_gain = split_score(prefix, whole)

time: 417 us -> 552 us (1.32)
  blocking collectives: 24.5 us -> 122 us
  waiting for transfers between devices: 74.4 us -> 118 us
  between operations: 14.3 us -> 0.91 us
  starting transfers between devices: 0.04 us -> 7.95 us
    ppermute x0 -> x4, waiting for transfers between devices: none -> 118 us  [on_device(): lax.ppermute(summed, 'rows', [(i, i ^ far) for i in range(count)])]
    all_gather x1, blocking collectives: 24.5 us -> 122 us  [on_device(): all_votes = lax.all_gather(feature_votes, 'rows', axis=0, tiled=True)]
    psum x1 -> x0, waiting for transfers between devices: 74.4 us -> none  [on_device(): summed = lax.psum(histogram, 'rows')]
    ppermute x0 -> x4, starting transfers between devices: none -> 7.95 us  [on_device(): lax.ppermute(summed, 'rows', [(i, i ^ far) for i in range(count)])]
  transfers between devices with their start and end apart: 1 -> 4, of which waited for: 1 -> 3; matrix products, arithmetic and copies ran while one was open for 1% -> 1% of each run, Pallas kernels for 0% -> 0%
where the time goes in v1:
time: 552 us; the launch traced here: 544 us
  local copies, waits for them, and re-layouts  189 us (34%)
  blocking collectives  122 us (22%)
  waiting for transfers between devices  118 us (21%)
  other arithmetic  94.4 us (17%)
  matrix products  10.5 us (2%)
  starting transfers between devices  7.95 us (1%)
    gather x5, local copies, waits for them, and re-layouts, build_histogram(): chosen = jnp.take_along_axis(feature_bin, columns, axis=1)  164 us
    all_gather x1, blocking collectives, on_device(): all_votes = lax.all_gather(feature_votes, 'rows', axis=0, tiled=True)  122 us
    ppermute x4, waiting for transfers between devices, on_device(): lax.ppermute(summed, 'rows', [(i, i ^ far) for i in range(count)])  118 us
    another operation x5, other arithmetic  72.3 us
  transfers between devices with their start and end apart: 4, of which 3 were waited for; matrix products, arithmetic and copies ran while one was open for 1% of the time, Pallas kernels for 0%

profile of v1, /device:TPU:0, one launch (start us, length us, event | category | flops | bytes accessed | tf_op | source)
XLA Modules:
  0.0 544.1 jit_solution(17703792115951882165)
XLA Ops:
  0.6 0.0 copy-start
  0.7 0.8 reshape.169
  1.5 0.7 reshape.170
  2.2 0.7 reshape.171
  2.9 9.2 %while.18 = (s32[]{:T(128)}, f32[2,256]{1,0:T(2,128)S(1)}, f32[2,256]{1,0:T(2,128)S(1)}, s32[2,256]{1,0:T(2,128)S(1)}, s32[2]{0:T(128)}, /*index=5*/f32[2,256]{1...) while((s32[]{:T(128)}, f32[2,256]{1,0:T(2,128)S(1)}, f32[2,256]{1,0:T(2,128)S(1)}, ...), condition=%wide.region_7.8_spmd, body=%wide.region_0.7_spmd.sunk | while | flops 2035203 | bytes 32681 | solution.py:88
  2.9 1.2 dynamic_slice.34
  4.1 0.6 iota_compare_fusion.6
  4.8 0.2 convert_reduce_fusion.3
  5.0 1.3 exponential_add_fusion.5
  7.0 0.4 fusion.29
  7.5 1.2 dynamic_slice.34
  8.7 0.6 iota_compare_fusion.6
  9.4 0.2 convert_reduce_fusion.3
  9.6 1.3 exponential_add_fusion.5
  11.6 0.4 fusion.29
  12.1 0.0 copy-start.3
  12.1 0.0 copy-start.4
  12.1 1.0 bitcast_or_fusion
  13.1 0.1 copy.34
  13.2 0.2 reshape.179
  13.4 0.0 copy-done
  13.4 0.0 copy-start.5
  13.4 163.1 %gather_fusion = s32[20480]{0:T(1024)S(1)} fusion(s32[512,700]{0,1:T(8,128)S(1)} %copy-done, s32[20480]{0:T(1024)S(1)} %reshape.179), kind=kCustom, calls=%fused_computation | custom fusion | bytes 327680 | tf_op jit(solution)/shard_map/jit(take_along_axis)/gather | solution.py:48
  176.5 0.2 reshape.182
  176.7 0.1 copy.35
  176.8 0.0 copy-done.3
  176.9 0.0 copy-done.4
  176.9 0.0 copy-done.5
  176.9 3.3 bitcast_compare_fusion
  180.3 9.5 %fusion.23 = f32[2,32,40,256]{3,1,2,0:T(8,128)S(1)} fusion(f32[2,32,512,1]{2,1,3,0:T(8,128)S(1)} %bitcast.69, pred[40,256,512,1]{2,1,0,3:T(32,128)(4,1)S(1)} %bitcast.68), kind=kOutput, calls=%fused_computation.57 | convolution fusion | flops 4026531840 | bytes 7995392 | tf_op jit(solution)/shard_map/while/body/eval_jaxpr/dot_general | solution.py:57
  189.8 0.6 collective-permute-start
  190.3 4.5 collective-permute-done
  194.9 0.5 add.113
  195.4 2.9 collective-permute-start.1
  198.3 57.2 %collective-permute-done.1 = f32[2,32,40,256]{3,1,2,0:T(8,128)S(1)} collective-permute-done((f32[2,32,40,256]{3,1,2,0:T(8,128)S(1)}, f32[2,32,40,256]{3,1,2,0:T(8,128)S(1)}, u32[]{:S(2)}, u32[]{:S(2)}) %collective-permute-start.1) | collective-permute-done | bytes 2621472 | tf_op jit(solution)/shard_map/ppermute | solution.py:103
  255.5 0.5 add.114
  256.0 0.0 copy-start.2
  256.0 1.9 collective-permute-start.2
  257.9 56.5 %collective-permute-done.2 = f32[2,32,40,256]{3,1,2,0:T(8,128)S(1)} collective-permute-done((f32[2,32,40,256]{3,1,2,0:T(8,128)S(1)}, f32[2,32,40,256]{3,1,2,0:T(8,128)S(1)}, u32[]{:S(2)}, u32[]{:S(2)}) %collective-permute-start.2) | collective-permute-done | bytes 2621472 | tf_op jit(solution)/shard_map/ppermute | solution.py:103
  314.4 0.8 add.115
  315.2 2.6 collective-permute-start.3
  317.8 0.0 copy-done.2
  317.8 121.9 %all_gather.3 = s32[16,32,20]{1,2,0:T(8,128)S(1)} all-gather(s32[1,32,20]{1,2,0:T(8,128)S(1)} %copy.33), channel_id=1, replica_groups=mesh['parts'=2,'rows'=16] {'rows'}, dimensions={0}, use_global_device_ids=true | all-gather | bytes 43520 | tf_op jit(solution)/shard_map/all_gather | solution.py:82
  439.7 4.4 convert_reduce_fusion.1
  444.1 0.0 collective-permute-done.3
  444.1 1.9 fusion.22
  446.0 0.1 copy.40
  446.1 4.3 reshape.175
  450.3 4.8 copy.36
  455.1 69.9 %reduce-window.6 = f32[2,32,40,2,128]{4,2,3,1,0:T(8,128)} reduce-window(f32[2,32,40,2,128]{4,2,3,1,0:T(8,128)} %copy.36, f32[]{:T(128)} %constant.79.clone.1), window={size=1x1x1x1x128 pad=0_0x0_0x0_0x0_0x127_0}, to_apply=%region_9.10 | reduce-window | flops 83230720 | bytes 5242884 | tf_op jit(solution)/shard_map/reduce-window
  525.0 4.0 slice.41
  529.0 2.7 copy.37
  531.7 0.2 fusion.14
  531.8 0.1 copy.38
  531.9 0.0 copy-start.1
  531.9 2.3 broadcast_add_fusion
  534.2 0.2 copy-done.1
  534.4 2.3 bitcast_subtract_fusion
  536.7 0.2 fusion.13
  536.9 1.7 copy.39
  538.6 2.3 div.58
  540.9 0.1 copy.42
  541.0 3.1 fusion.12
  (24 shorter events, 0.3 us)
Async XLA Ops:
  0.6 12.8 %copy-start = (s32[512,700]{0,1:T(8,128)S(1)}, s32[512,700]{0,1:T(8,128)}, u32[]{:S(2)}) copy-start(s32[512,700]{0,1:T(8,128)} %param.10) | copy-start | bytes 4300804
  12.1 164.8 %copy-start.3 = (f32[1,2,2,128]{3,1,2,0:T(2,128)}, f32[1,2,2,128]{3,1,2,0:T(2,128)S(1)}, u32[]{:S(2)}) copy-start(f32[1,2,2,128]{3,1,2,0:T(2,128)S(1)} %copy.45) | copy-start | bytes 6148
  12.1 164.8 %copy-start.4 = (f32[1,2,2,128]{3,1,2,0:T(2,128)}, f32[1,2,2,128]{3,1,2,0:T(2,128)S(1)}, u32[]{:S(2)}) copy-start(f32[1,2,2,128]{3,1,2,0:T(2,128)S(1)} %copy.46) | copy-start | bytes 6148
  13.4 163.4 %copy-start.5 = (s32[512]{0:T(512)S(1)}, s32[512]{0:T(512)}, u32[]{:S(2)}) copy-start(s32[512]{0:T(512)} %param.11) | copy-start | bytes 6148
  189.8 5.1 collective-permute-start
  195.4 60.1 %collective-permute-start.1 = (f32[2,32,40,256]{3,1,2,0:T(8,128)S(1)}, f32[2,32,40,256]{3,1,2,0:T(8,128)S(1)}, u32[]{:S(2)}, u32[]{:S(2)}) collective-permute-start(f32[2,32,40,256]{3,1,2,0:T(8,128)S(1)} %add.113), channel_id=1, source_target_pairs={{0,2},{1,3},{2,0},{3,1},{4,6},{5,7},{6,4},{7,5},{8,10},{9,11},{10,... | collective-permute-start | bytes 7864328 | tf_op jit(solution)/shard_map/ppermute | solution.py:103
  256.0 61.8 %copy-start.2 = (s32[1,32,20]{1,0,2:T(1,128)S(1)}, s32[1,32,20]{1,0,2:T(1,128)}, u32[]{:S(2)}) copy-start(s32[1,32,20]{1,0,2:T(1,128)} %param.16) | copy-start | bytes 7684
  256.0 58.4 %collective-permute-start.2 = (f32[2,32,40,256]{3,1,2,0:T(8,128)S(1)}, f32[2,32,40,256]{3,1,2,0:T(8,128)S(1)}, u32[]{:S(2)}, u32[]{:S(2)}) collective-permute-start(f32[2,32,40,256]{3,1,2,0:T(8,128)S(1)} %add.114), channel_id=1, source_target_pairs={{0,4},{1,5},{2,6},{3,7},{4,0},{5,1},{6,2},{7,3},{8,12},{9,13},{10,... | collective-permute-start | bytes 7864328 | tf_op jit(solution)/shard_map/ppermute | solution.py:103
  315.2 128.9 %collective-permute-start.3 = (f32[2,32,40,256]{3,1,2,0:T(8,128)S(1)}, f32[2,32,40,256]{3,1,2,0:T(8,128)S(1)}, u32[]{:S(2)}, u32[]{:S(2)}) collective-permute-start(f32[2,32,40,256]{3,1,2,0:T(8,128)S(1)} %add.115), channel_id=1, source_target_pairs={{0,8},{1,9},{2,10},{3,11},{4,12},{5,13},{6,14},{7,15},{8,0},{9,1},... | collective-permute-start | bytes 7864328 | tf_op jit(solution)/shard_map/ppermute | solution.py:103
  531.9 2.5 copy-start.1
